TPU v7x, 128 devices: a whole 4x4x4 slice. The times are simulated.
128 devices in a mesh: rep: 4 (over x_hi, core), tp: 32 (over z, x_lo, y).
Axes of the slice: x: 4 (x_hi: 2, x_lo: 2; x = x_hi * 2 + x_lo), y: 4, z: 4, core: 2. Of those that a mesh axis runs over, the one named last changes fastest.
Arguments:
- trainer_query: float32 [128, 64, 8192], P(('rep', 'tp')), may hold values from -6 to 6
- trainer_output: float32 [128, 8192, 64], P(('rep', 'tp')), may hold values from -6 to 6
- probes: bfloat16 [768, 8192], replicated, may hold values from -0.0625 to 0.0625
- shard_block: int32 [128], replicated, may hold values from 0 to 127, each once
- slice_owner: int32 [32], replicated, may hold values from 0 to 31, each once
Outputs:
- query_slices: bfloat16 [32, 8192, 256], P('tp')
- output_slices: bfloat16 [32, 256, 8192], P('tp')
- query_prints: float32 [32, 768, 256], P('tp')
- output_prints: float32 [32, 256, 768], P('tp')
Inputs may be any that keep to these rules, and one draw needn't show every extreme that they name: `shard_block`: a permutation: each number once. `slice_owner`: a permutation: each number once.
All inputs are finite; a program needn't handle non-finite values.
Results may differ from a plain program's by a relative error of at most 0.0029.
Values may be sent and summed in bfloat16 or wider, within the bound.
A program may use at most 128 MiB of HBM per device.

v0:
```python
import jax
import jax.numpy as jnp
from jax import lax
from jax.sharding import PartitionSpec as P


def cut_along(shard, dim, length):
    dims = shard.shape
    pieces = shard.reshape(*dims[:dim], length, dims[dim] // length, *dims[dim + 1 :])
    return jnp.moveaxis(pieces, dim, 0)


def edges_of(length, count):
    unit = 8 if length >= 8 * count else 1
    return [length // unit * k // count * unit for k in range(1, count)]


def laid_out(pieces, dim):
    pieces = jnp.moveaxis(pieces, 0, dim)
    dims = pieces.shape
    return pieces.reshape(*dims[:dim], dims[dim] * dims[dim + 1], *dims[dim + 2 :])


def cut_exchange(shard, axis, pieces, split_dim, concat_dim):
    blocks = cut_along(shard, split_dim, lax.axis_size(axis))
    split_at = max(range(1, max(2, blocks.ndim - 1)), key=lambda d: blocks.shape[d])
    outs = []
    for section in jnp.split(blocks, edges_of(blocks.shape[split_at], pieces), axis=split_at):
        if section.size:
            outs.append(lax.all_to_all(section, axis, split_axis=0, concat_axis=0, tiled=True))
    return laid_out(jnp.concatenate(outs, axis=split_at), concat_dim)


def per_device(trainer_query, trainer_output, probes, shard_block, slice_owner):
    tp_count = lax.axis_size("tp")
    rep_count = lax.axis_size("rep")
    dev_count = tp_count * rep_count
    shard_rows = trainer_query.shape[1]
    query_width = trainer_query.shape[2]
    slice_width = query_width // tp_count
    model_width = shard_rows * dev_count
    positions = jnp.arange(dev_count, dtype=jnp.int32)
    inverse = jnp.zeros((dev_count,), jnp.int32).at[shard_block].set(positions)
    query_local = trainer_query[0].astype(jnp.bfloat16)
    query_blocks = jnp.take(
        query_local.reshape(shard_rows, tp_count, slice_width), slice_owner, axis=1
    ).reshape(shard_rows, query_width)
    output_local = trainer_output[0].astype(jnp.bfloat16)
    output_blocks = jnp.take(
        output_local.reshape(tp_count, slice_width, shard_rows), slice_owner, axis=0
    ).reshape(query_width, shard_rows)
    query_moved = lax.all_to_all(query_blocks, "tp", split_axis=1, concat_axis=0, tiled=True)
    query_all = lax.all_gather(query_moved, "rep", axis=0, tiled=True)
    output_moved = cut_exchange(output_blocks, "tp", 2, 0, 1)
    output_all = lax.all_gather(output_moved, "rep", axis=1, tiled=True)
    query_ordered = query_all.reshape(dev_count, shard_rows, slice_width)
    query_slice = jnp.take(query_ordered, inverse, axis=0).reshape(model_width, slice_width)
    output_ordered = output_all.reshape(slice_width, dev_count, shard_rows)
    output_slice = jnp.take(output_ordered, inverse, axis=1).reshape(slice_width, model_width)
    query_prints = jnp.dot(probes, query_slice, preferred_element_type=jnp.float32)
    output_prints = lax.dot_general(
        output_slice, probes, (((1,), (1,)), ((), ())), preferred_element_type=jnp.float32
    )
    return (query_slice[None], output_slice[None], query_prints[None], output_prints[None])


def solution(mesh):
    placed = (P(("rep", "tp"), None, None), P(("rep", "tp"), None, None), P(), P(), P())
    return jax.shard_map(
        per_device,
        mesh=mesh,
        in_specs=placed,
        out_specs=(
            P("tp", None, None),
            P("tp", None, None),
            P("tp", None, None),
            P("tp", None, None),
        ),
        check_vma=False,
    )
```

profile of v0, /device:TPU:1, one launch (start us, length us, event | category | flops | bytes accessed | tf_op | source)
XLA Modules:
  0.0 165.8 jit_solution(11763954619681203649)
XLA Ops:
  7.2 0.7 compare_select_fusion
  7.9 0.7 compare_and_fusion
  8.5 1.7 %convert_element_type.16 = bf16[1,8192,64]{1,2,0:T(8,128)(2,1)S(1)} convert(f32[1,8192,64]{1,2,0:T(8,128)} %param.6) | non-fusion elementwise | flops 524288 | bytes 3145728 | tf_op jit(solution)/shard_map/convert_element_type | solution.py:48
  10.5 0.6 copy.13
  11.1 0.6 gather_fusion.2
  12.2 19.7 %all_to_all.26 = bf16[32,128,64]{1,2,0:T(8,128)(2,1)S(1)} all-to-all(bf16[32,128,64]{1,2,0:T(8,128)(2,1)S(1)} %get-tuple-element.16), channel_id=1, replica_groups=mesh['rep'=4,'tp'=32] {'tp'}, dimensions={0} | all-to-all | bytes 1048576 | tf_op jit(solution)/shard_map/all_to_all | solution.py:30
  31.9 15.4 %all_to_all.27 = bf16[32,128,64]{1,2,0:T(8,128)(2,1)S(1)} all-to-all(bf16[32,128,64]{1,2,0:T(8,128)(2,1)S(1)} %get-tuple-element.17), channel_id=1, replica_groups=mesh['rep'=4,'tp'=32] {'tp'}, dimensions={0} | all-to-all | bytes 1048576 | tf_op jit(solution)/shard_map/all_to_all | solution.py:30
  47.2 1.1 pad_maximum_fusion
  48.8 0.6 copy.12
  49.4 0.6 gather_fusion
  50.2 27.8 %all_to_all.28 = bf16[64,32,256]{2,0,1:T(8,128)(2,1)} all-to-all(bf16[64,32,256]{2,0,1:T(8,128)(2,1)S(1)} %select_bitcast_fusion), channel_id=1, replica_groups=mesh['rep'=4,'tp'=32] {'tp'}, dimensions={1} | all-to-all | bytes 2097152 | tf_op jit(solution)/shard_map/all_to_all | solution.py:52
  78.1 1.2 scatter_custom_fusion
  79.5 15.6 %all-gather.5.cloned.1.call-done = bf16[256,8192]{0,1:T(8,128)(2,1)} async-done(((bf16[256,2048]{0,1:T(8,128)(2,1)}), bf16[256,8192]{0,1:T(8,128)(2,1)}) %all-gather.5.cloned.1.call-update) | async-done | bytes 4194320 | tf_op jit(solution)/shard_map/all_gather | solution.py:55
  95.1 5.0 %gather_fusion.3 = bf16[128,256,64]{1,2,0:T(8,128)(2,1)} fusion(bf16[256,128,64]{0,2,1:T(8,128)(2,1)} %bitcast.43, s32[1024]{0:T(1024)S(1)} %pad_clamp_fusion), kind=kCustom, calls=%fused_computation.3 | custom fusion | bytes 8389120 | tf_op jit(solution)/shard_map/jit(_take)/gather | solution.py:59
  100.1 5.3 %bitcast_select_fusion.1 = bf16[1,256,8192]{1,2,0:T(8,128)(2,1)} fusion(pred[8192]{0:T(1024)(128)(4,1)S(1)} %broadcast_in_dim.67, bf16[1,256,8192]{1,2,0:T(8,128)(2,1)} %bitcast.41), kind=kLoop, calls=%fused_computation.6 | loop fusion | flops 2097152 | bytes 8396800 | tf_op jit(solution)/shard_map/jit(_take)/select_n | solution.py:59
  105.3 6.5 %copy.14 = bf16[1,256,8192]{2,1,0:T(8,128)(2,1)} copy(bf16[1,256,8192]{1,2,0:T(8,128)(2,1)} %bitcast_select_fusion.1) | data formatting | bytes 8388608
  111.8 6.0 %bitcast_select_fusion = bf16[256,8192]{0,1:T(8,128)(2,1)S(1)} fusion(bf16[128,256,64]{1,2,0:T(8,128)(2,1)} %gather_fusion.3, pred[8192]{0:T(1024)(128)(4,1)S(1)} %broadcast_in_dim.67), kind=kLoop, calls=%fused_computation.5 | loop fusion | flops 2097152 | bytes 8396800 | tf_op jit(solution)/shard_map/jit(_take)/select_n | solution.py:59
  117.8 7.4 %convolution_bitcast_fusion = f32[1,256,768]{2,1,0:T(8,128)} fusion(bf16[256,8192]{0,1:T(8,128)(2,1)S(1)} %bitcast_select_fusion, bf16[768,8192]{1,0:T(8,128)(2,1)} %param.7), kind=kOutput, calls=%fused_computation.9 | convolution fusion | flops 3221225472 | bytes 17563648 | tf_op jit(solution)/shard_map/dot_general | solution.py:61
  125.2 9.8 %all-gather.3.cloned.1.call-done = bf16[8192,256]{1,0:T(8,128)(2,1)} async-done(((bf16[2048,256]{1,0:T(8,128)(2,1)}), bf16[8192,256]{1,0:T(8,128)(2,1)}) %all-gather.3.cloned.1.call-update) | async-done | bytes 4194320 | tf_op jit(solution)/shard_map/all_gather | solution.py:53
  135.0 5.0 %gather_fusion.1 = bf16[128,64,256]{2,1,0:T(8,128)(2,1)} fusion(bf16[128,64,256]{2,1,0:T(8,128)(2,1)} %bitcast.46, s32[1024]{0:T(1024)S(1)} %pad_clamp_fusion), kind=kCustom, calls=%fused_computation.1 | custom fusion | bytes 8389120 | tf_op jit(solution)/shard_map/jit(_take)/gather | solution.py:57
  140.1 6.0 %bitcast_select_fusion.2 = bf16[8192,256]{1,0:T(8,128)(2,1)S(1)} fusion(bf16[128,64,256]{2,1,0:T(8,128)(2,1)} %gather_fusion.1, pred[8192]{0:T(1024)(128)(4,1)S(1)} %broadcast_in_dim.67), kind=kLoop, calls=%fused_computation.7 | loop fusion | flops 2097152 | bytes 8396800 | tf_op jit(solution)/shard_map/jit(_take)/select_n | solution.py:57
  146.0 6.5 %convolution_bitcast_fusion.1 = f32[1,768,256]{1,2,0:T(8,128)S(1)} fusion(bf16[8192,256]{1,0:T(8,128)(2,1)S(1)} %bitcast_select_fusion.2, bf16[768,8192]{1,0:T(8,128)(2,1)} %param.7), kind=kOutput, calls=%fused_computation.10 | convolution fusion | flops 3221225472 | bytes 17563648 | tf_op jit(solution)/shard_map/dot_general | solution.py:60
  152.6 1.1 copy.15
  153.7 5.2 %bitcast_select_fusion.3 = bf16[1,8192,256]{2,1,0:T(8,128)(2,1)} fusion(pred[8192]{0:T(1024)(128)(4,1)S(1)} %broadcast_in_dim.67, bf16[1,8192,256]{2,1,0:T(8,128)(2,1)} %bitcast.42), kind=kLoop, calls=%fused_computation.8 | loop fusion | flops 2097152 | bytes 8396800 | tf_op jit(solution)/shard_map/jit(_take)/select_n | solution.py:57
  (22 shorter events, 1.6 us)
Async XLA Ops:
  7.2 87.9 %all-gather.5.cloned.1.call-start = ((), (), s32[]{:S(2)}) async-start(), calls=%async_computation.4 | async-start | bytes 5242880 | tf_op jit(solution)/shard_map/all_gather | solution.py:55
  11.9 36.5 %copy-start = (f32[1,64,8192]{2,1,0:T(8,128)S(1)}, f32[1,64,8192]{2,1,0:T(8,128)}, u32[]{:S(2)}) copy-start(f32[1,64,8192]{2,1,0:T(8,128)} %param.5) | copy-start | bytes 6291460
  48.4 86.7 %all-gather.3.cloned.1.call-start = ((), (), s32[]{:S(2)}) async-start(), calls=%async_computation.3 | async-start | bytes 5242880 | tf_op jit(solution)/shard_map/all_gather | solution.py:53
  49.4 28.7 %copy-start.1 = (s32[128]{0:T(128)S(1)}, s32[128]{0:T(128)}, u32[]{:S(2)}) copy-start(s32[128]{0:T(128)} %param.8) | copy-start | bytes 1540
Sparse Core Ops, SparseCore 0:
  48.5 46.5 all-gather.4
  96.7 38.2 all-gather.2
where the time goes:
time: 167 us; the launch traced here: 166 us
  blocking collectives  62.9 us (38%)
  other arithmetic  27 us (16%)
  waiting for transfers between devices  25.4 us (15%)
  local copies, waits for them, and re-layouts  22.2 us (13%)
  between operations  14.2 us (9%)
  matrix products  13.9 us (8%)
    all_to_all x2, blocking collectives, cut_exchange(): lax.all_to_all(section, axis, split_axis=0, concat_axis=0, tiled=True)  35 us
    all_to_all x1, blocking collectives, per_device(): lax.all_to_all(query_blocks, 'tp', split_axis=1, concat_axis=0, tiled=True)  27.8 us
    all_gather x1, waiting for transfers between devices, per_device(): output_all = lax.all_gather(output_moved, 'rep', axis=1, tiled=True)  15.6 us
    select_n x2, other arithmetic, per_device(): jnp.take(output_ordered, inverse, axis=1).reshape(slice_width, model_width)  11.2 us
    select_n x3, other arithmetic, per_device(): jnp.take(query_ordered, inverse, axis=0).reshape(model_width, slice_width)  11.2 us
    all_gather x1, waiting for transfers between devices, per_device(): query_all = lax.all_gather(query_moved, 'rep', axis=0, tiled=True)  9.84 us
    unnamed x8, local copies, waits for them, and re-layouts  8.14 us
    dot_general x1, matrix products, per_device(): lax.dot_general(output_slice, probes, (((1,), (1,)), ((), ())), preferred...  7.43 us
  transfers between devices with their start and end apart: 2, of which 2 were waited for; matrix products, arithmetic and copies ran while one was open for 20% of the time, Pallas kernels for 0%

commit v1 on v0

--- a/solution.py
+++ b/solution.py
@@ -52,7 +52,10 @@
     query_moved = lax.all_to_all(query_blocks, "tp", split_axis=1, concat_axis=0, tiled=True)
     query_all = lax.all_gather(query_moved, "rep", axis=0, tiled=True)
     output_moved = cut_exchange(output_blocks, "tp", 2, 0, 1)
-    output_all = lax.all_gather(output_moved, "rep", axis=1, tiled=True)
+    devices = lax.axis_size("rep")
+    shards = jnp.stack([output_moved for _ in range(devices)])
+    shards = lax.all_to_all(shards, "rep", split_axis=0, concat_axis=0)
+    output_all = jnp.concatenate(shards, axis=1)
     query_ordered = query_all.reshape(dev_count, shard_rows, slice_width)
     query_slice = jnp.take(query_ordered, inverse, axis=0).reshape(model_width, slice_width)
     output_ordered = output_all.reshape(slice_width, dev_count, shard_rows)

time: 167 us -> 212 us (1.27)
  waiting for transfers between devices: 25.4 us -> 90.9 us
  blocking collectives: 62.9 us -> 19.6 us
  starting transfers between devices: 0.08 us -> 18.8 us
  local copies, waits for them, and re-layouts: 22.2 us -> 25.2 us
    all_to_all x0 -> x3, waiting for transfers between devices: none -> 90.2 us  [the longest x1 69.1 us: per_device(): shards = lax.all_to_all(shards, 'rep', split_axis=0, concat_axis=0)]
    all_to_all x1 -> x0, blocking collectives: 27.8 us -> none  [per_device(): lax.all_to_all(query_blocks, 'tp', split_axis=1, concat_axis=0, tiled=True)]
    all_to_all x0 -> x3, starting transfers between devices: none -> 18.8 us  [the longest x1 6.92 us: per_device(): shards = lax.all_to_all(shards, 'rep', split_axis=0, concat_axis=0)]
    all_gather x1 -> x0, waiting for transfers between devices: 15.6 us -> none  [per_device(): output_all = lax.all_gather(output_moved, 'rep', axis=1, tiled=True)]
    all_to_all x2 -> x1, blocking collectives: 35 us -> 19.6 us  [cut_exchange(): lax.all_to_all(section, axis, split_axis=0, concat_axis=0, tiled=True)]
    all_gather x1, waiting for transfers between devices: 9.84 us -> 0.01 us  [per_device(): query_all = lax.all_gather(query_moved, 'rep', axis=0, tiled=True)]
    another operation x0 -> x1, local copies, waits for them, and re-layouts: none -> 2.36 us  [per_device(): shards = jnp.stack([output_moved for _ in range(devices)])]
    unnamed x8 -> x12, local copies, waits for them, and re-layouts: 8.14 us -> 7.99 us
  transfers between devices with their start and end apart: 2 -> 4, of which waited for: 2 -> 3; matrix products, arithmetic and copies ran while one was open for 20% -> 17% of each run, Pallas kernels for 0% -> 0%
where the time goes in v1:
time: 212 us; the launch traced here: 211 us
  waiting for transfers between devices  90.9 us (43%)
  other arithmetic  28.1 us (13%)
  local copies, waits for them, and re-layouts  25.2 us (12%)
  blocking collectives  19.6 us (9%)
  starting transfers between devices  18.8 us (9%)
  between operations  14.2 us (7%)
  matrix products  13.9 us (7%)
    all_to_all x1, waiting for transfers between devices, per_device(): shards = lax.all_to_all(shards, 'rep', split_axis=0, concat_axis=0)  69.1 us
    all_to_all x1, blocking collectives, cut_exchange(): lax.all_to_all(section, axis, split_axis=0, concat_axis=0, tiled=True)  19.6 us
    all_to_all x1, waiting for transfers between devices, per_device(): lax.all_to_all(query_blocks, 'tp', split_axis=1, concat_axis=0, tiled=True)  14.1 us
    select_n x2, other arithmetic, per_device(): jnp.take(output_ordered, inverse, axis=1).reshape(slice_width, model_width)  11.2 us
    select_n x3, other arithmetic, per_device(): jnp.take(query_ordered, inverse, axis=0).reshape(model_width, slice_width)  11.2 us
    unnamed x12, local copies, waits for them, and re-layouts  7.99 us
    dot_general x1, matrix products, per_device(): lax.dot_general(output_slice, probes, (((1,), (1,)), ((), ())), preferred...  7.38 us
    all_to_all x1, waiting for transfers between devices, cut_exchange(): lax.all_to_all(section, axis, split_axis=0, concat_axis=0, tiled=True)  6.98 us
  transfers between devices with their start and end apart: 4, of which 3 were waited for; matrix products, arithmetic and copies ran while one was open for 17% of the time, Pallas kernels for 0%

profile of v1, /device:TPU:1, one launch (start us, length us, event | category | flops | bytes accessed | tf_op | source)
XLA Modules:
  0.0 210.8 jit_solution(13686621969802074042)
XLA Ops:
  8.5 1.7 convert_element_type.16
  11.9 1.1 fusion.2
  13.0 19.6 %all_to_all.31 = bf16[32,128,64]{1,2,0:T(8,128)(2,1)} all-to-all(bf16[32,128,64]{1,2,0:T(8,128)(2,1)S(1)} %get-tuple-element.16), channel_id=1, replica_groups=mesh['rep'=4,'tp'=32] {'tp'}, dimensions={0} | all-to-all | bytes 1048576 | tf_op jit(solution)/shard_map/all_to_all | solution.py:30
  32.6 5.9 %all-to-all-start.2 = ((bf16[32,128,64]{1,2,0:T(8,128)(2,1)}), bf16[32,128,64]{1,2,0:T(8,128)(2,1)}, u32[]{:S(2)}, u32[]{:S(2)}) async-start(bf16[32,128,64]{1,2,0:T(8,128)(2,1)} %get-tuple-element.17), calls=%async_computation.2 | async-start | bytes 1048576 | tf_op jit(solution)/shard_map/all_to_all | solution.py:30
  40.2 1.1 select_bitcast_fusion
  41.3 7.0 %all-to-all-done.2 = bf16[32,128,64]{1,2,0:T(8,128)(2,1)} async-done(((bf16[32,128,64]{1,2,0:T(8,128)(2,1)}), bf16[32,128,64]{1,2,0:T(8,128)(2,1)}, u32[]{:S(2)}, u32[]{:S(2)}) %all-to-all-start.2) | async-done | bytes 524320 | tf_op jit(solution)/shard_map/all_to_all | solution.py:30
  48.3 5.9 %all-to-all-start = ((bf16[64,32,256]{2,0,1:T(8,128)(2,1)}), bf16[64,32,256]{2,0,1:T(8,128)(2,1)S(1)}, u32[]{:S(2)}, u32[]{:S(2)}) async-start(bf16[64,32,256]{2,0,1:T(8,128)(2,1)} %select_bitcast_fusion), calls=%async_computation | async-start | bytes 2097152 | tf_op jit(solution)/shard_map/all_to_all | solution.py:52
  54.2 1.2 pad_maximum_fusion
  55.4 14.1 %all-to-all-done = bf16[64,32,256]{2,0,1:T(8,128)(2,1)S(1)} async-done(((bf16[64,32,256]{2,0,1:T(8,128)(2,1)}), bf16[64,32,256]{2,0,1:T(8,128)(2,1)S(1)}, u32[]{:S(2)}, u32[]{:S(2)}) %all-to-all-start) | async-done | bytes 1048608 | tf_op jit(solution)/shard_map/all_to_all | solution.py:52
  69.6 2.4 %stack.3 = bf16[4,256,2048]{1,2,0:T(8,128)(2,1)} broadcast(bf16[256,2048]{0,1:T(8,128)(2,1)S(1)} %bitcast.45), dimensions={1,2} | broadcast | bytes 5242880 | tf_op jit(solution)/shard_map/stack | solution.py:56
  71.9 6.9 %all-to-all-start.3 = ((bf16[4,256,2048]{1,2,0:T(8,128)(2,1)}), bf16[4,256,2048]{1,2,0:T(8,128)(2,1)}, u32[]{:S(2)}, u32[]{:S(2)}) async-start(bf16[4,256,2048]{1,2,0:T(8,128)(2,1)} %stack.3), calls=%async_computation.3 | async-start | bytes 8388608 | tf_op jit(solution)/shard_map/all_to_all | solution.py:57
  78.9 0.7 all-gather.2.cloned.1.call-update
  79.6 1.2 scatter_custom_fusion
  81.0 69.1 %all-to-all-done.3 = bf16[4,256,2048]{1,2,0:T(8,128)(2,1)} async-done(((bf16[4,256,2048]{1,2,0:T(8,128)(2,1)}), bf16[4,256,2048]{1,2,0:T(8,128)(2,1)}, u32[]{:S(2)}, u32[]{:S(2)}) %all-to-all-start.3) | async-done | bytes 4194336 | tf_op jit(solution)/shard_map/all_to_all | solution.py:57
  150.1 5.0 %gather_fusion.3 = bf16[128,256,64]{1,2,0:T(8,128)(2,1)} fusion(bf16[256,128,64]{0,2,1:T(8,128)(2,1)} %bitcast.8, s32[1024]{0:T(1024)S(1)} %pad_clamp_fusion), kind=kCustom, calls=%fused_computation.3 | custom fusion | bytes 8389120 | tf_op jit(solution)/shard_map/jit(_take)/gather | solution.py:62
  155.1 5.3 %bitcast_select_fusion.1 = bf16[1,256,8192]{1,2,0:T(8,128)(2,1)} fusion(pred[8192]{0:T(1024)(128)(4,1)S(1)} %broadcast_in_dim.67, bf16[1,256,8192]{1,2,0:T(8,128)(2,1)} %bitcast.43), kind=kLoop, calls=%fused_computation.6 | loop fusion | flops 2097152 | bytes 8396800 | tf_op jit(solution)/shard_map/jit(_take)/select_n | solution.py:62
  160.4 6.3 %copy.14 = bf16[1,256,8192]{2,1,0:T(8,128)(2,1)} copy(bf16[1,256,8192]{1,2,0:T(8,128)(2,1)} %bitcast_select_fusion.1) | data formatting | bytes 8388608
  166.7 6.0 %bitcast_select_fusion = bf16[256,8192]{0,1:T(8,128)(2,1)S(1)} fusion(bf16[128,256,64]{1,2,0:T(8,128)(2,1)} %gather_fusion.3, pred[8192]{0:T(1024)(128)(4,1)S(1)} %broadcast_in_dim.67), kind=kLoop, calls=%fused_computation.5 | loop fusion | flops 2097152 | bytes 8396800 | tf_op jit(solution)/shard_map/jit(_take)/select_n | solution.py:62
  172.7 7.4 %convolution_bitcast_fusion = f32[1,256,768]{2,1,0:T(8,128)} fusion(bf16[256,8192]{0,1:T(8,128)(2,1)S(1)} %bitcast_select_fusion, bf16[768,8192]{1,0:T(8,128)(2,1)} %param.7), kind=kOutput, calls=%fused_computation.9 | convolution fusion | flops 3221225472 | bytes 17563648 | tf_op jit(solution)/shard_map/dot_general | solution.py:64
  180.1 5.0 %gather_fusion.1 = bf16[128,64,256]{2,1,0:T(8,128)(2,1)} fusion(bf16[128,64,256]{2,1,0:T(8,128)(2,1)} %bitcast.48, s32[1024]{0:T(1024)S(1)} %pad_clamp_fusion), kind=kCustom, calls=%fused_computation.1 | custom fusion | bytes 8389120 | tf_op jit(solution)/shard_map/jit(_take)/gather | solution.py:60
  185.1 6.0 %bitcast_select_fusion.2 = bf16[8192,256]{1,0:T(8,128)(2,1)S(1)} fusion(bf16[128,64,256]{2,1,0:T(8,128)(2,1)} %gather_fusion.1, pred[8192]{0:T(1024)(128)(4,1)S(1)} %broadcast_in_dim.67), kind=kLoop, calls=%fused_computation.7 | loop fusion | flops 2097152 | bytes 8396800 | tf_op jit(solution)/shard_map/jit(_take)/select_n | solution.py:60
  191.0 6.5 %convolution_bitcast_fusion.1 = f32[1,768,256]{1,2,0:T(8,128)S(1)} fusion(bf16[8192,256]{1,0:T(8,128)(2,1)S(1)} %bitcast_select_fusion.2, bf16[768,8192]{1,0:T(8,128)(2,1)} %param.7), kind=kOutput, calls=%fused_computation.10 | convolution fusion | flops 3221225472 | bytes 17563648 | tf_op jit(solution)/shard_map/dot_general | solution.py:63
  197.6 1.1 copy.15
  198.7 5.2 %bitcast_select_fusion.3 = bf16[1,8192,256]{2,1,0:T(8,128)(2,1)} fusion(pred[8192]{0:T(1024)(128)(4,1)S(1)} %broadcast_in_dim.67, bf16[1,8192,256]{2,1,0:T(8,128)(2,1)} %bitcast.44), kind=kLoop, calls=%fused_computation.8 | loop fusion | flops 2097152 | bytes 8396800 | tf_op jit(solution)/shard_map/jit(_take)/select_n | solution.py:60
  (28 shorter events, 4.7 us)
Async XLA Ops:
  11.7 26.9 %copy-start.1 = (f32[1,64,8192]{2,1,0:T(8,128)S(1)}, f32[1,64,8192]{2,1,0:T(8,128)}, u32[]{:S(2)}) copy-start(f32[1,64,8192]{2,1,0:T(8,128)} %param.5) | copy-start | bytes 6291460
  32.6 15.7 %all-to-all-start.2 = ((bf16[32,128,64]{1,2,0:T(8,128)(2,1)}), bf16[32,128,64]{1,2,0:T(8,128)(2,1)}, u32[]{:S(2)}, u32[]{:S(2)}) async-start(bf16[32,128,64]{1,2,0:T(8,128)(2,1)} %get-tuple-element.17), calls=%async_computation.2 | async-start | bytes 1048576 | tf_op jit(solution)/shard_map/all_to_all | solution.py:30
  38.9 15.3 %copy-start.2 = (bf16[32,128,64]{1,2,0:T(8,128)(2,1)S(1)}, bf16[32,128,64]{1,2,0:T(8,128)(2,1)}, u32[]{:S(2)}) copy-start(bf16[32,128,64]{1,2,0:T(8,128)(2,1)} %all_to_all.31) | copy-start | bytes 1572868
  48.3 21.3 %all-to-all-start = ((bf16[64,32,256]{2,0,1:T(8,128)(2,1)}), bf16[64,32,256]{2,0,1:T(8,128)(2,1)S(1)}, u32[]{:S(2)}, u32[]{:S(2)}) async-start(bf16[64,32,256]{2,0,1:T(8,128)(2,1)} %select_bitcast_fusion), calls=%async_computation | async-start | bytes 2097152 | tf_op jit(solution)/shard_map/all_to_all | solution.py:52
  69.6 2.4 %copy-start = (bf16[64,32,256]{2,0,1:T(8,128)(2,1)}, bf16[64,32,256]{2,0,1:T(8,128)(2,1)S(1)}, u32[]{:S(2)}) copy-start(bf16[64,32,256]{2,0,1:T(8,128)(2,1)S(1)} %all-to-all-done) | copy-start | bytes 3145732
  71.9 7.6 %copy-start.3 = (s32[128]{0:T(128)S(1)}, s32[128]{0:T(128)}, u32[]{:S(2)}) copy-start(s32[128]{0:T(128)} %param.8) | copy-start | bytes 1540
  71.9 78.2 %all-to-all-start.3 = ((bf16[4,256,2048]{1,2,0:T(8,128)(2,1)}), bf16[4,256,2048]{1,2,0:T(8,128)(2,1)}, u32[]{:S(2)}, u32[]{:S(2)}) async-start(bf16[4,256,2048]{1,2,0:T(8,128)(2,1)} %stack.3), calls=%async_computation.3 | async-start | bytes 8388608 | tf_op jit(solution)/shard_map/all_to_all | solution.py:57
  78.8 101.2 %all-gather.2.cloned.1.call-start = ((), (), s32[]{:S(2)}) async-start(), calls=%async_computation.4 | async-start | bytes 5242880 | tf_op jit(solution)/shard_map/all_gather | solution.py:53
Sparse Core Ops, SparseCore 0:
  81.3 60.5 all-gather.1
